TPU v7x, 32 devices: a whole 2x2x4 slice. The times are simulated.
32 devices in a mesh: subj: 4 (over y, core), vox: 8 (over z, x).
Axes of the slice: x: 2, y: 2, z: 4, core: 2. Of those that a mesh axis runs over, the one named last changes fastest.
Arguments:
- series: bfloat16 [16, 256, 16384], P('subj', None, 'vox'), may hold values from -6 to 6
- offsets: int32 [16, 12], replicated, may hold values from 0 to 240
- selected: int32 [16], replicated, may hold values from 0 to 16383, as said below
Outputs:
- kernel: float32 [16, 192, 192], P('vox', 'subj')
Inputs may be any that keep to these rules, and one draw needn't show every extreme that they name: `offsets`: each epoch lies inside its subject's run; epochs may intersect. `selected`: the ids are distinct.
All inputs are finite; a program needn't handle non-finite values.
Results may differ from a plain program's by a relative error of at most 0.00035.
Values may be sent and summed in bfloat16 or wider, within the bound.
A program may use at most 128 MiB of HBM per device.

v0:
```python
import functools

import jax
import jax.numpy as jnp
from jax import lax
from jax.experimental import pallas as pl
from jax.experimental.pallas import tpu as pltpu
from jax.sharding import PartitionSpec as P

TR = 16
KB = 8
C1 = 4
series_floor = 1.0
spread_floor = 0.05
shrink_factor = 0.9
f32 = jnp.float32
bf16 = jnp.bfloat16
MESH = pl.DeviceIdType.MESH


def iota(shape, dim):
    return lax.broadcasted_iota(jnp.int32, shape, dim)


def up8(n):
    return -(-n // 8) * 8


def pieces_of(G, V, NE):
    R = V
    while R > G and (V % R or R % G or (G * NE) % R or (G * NE // R) % 8):
        R -= 1
    return R


def column_groups(chunks):
    cuts = list(range(1, chunks, 2)) + [chunks]
    return tuple(zip(cuts[:-1], cuts[1:]))


def row_cuts(KI, NR, BR):
    return [0] + [min(up8((i + 1) * NR), BR) for i in range(KI)]


def flip(v, m):
    bit = 1
    while bit <= m:
        if m & bit:
            v = v + bit - 2 * bit * lax.rem(v // bit, 2)
        bit *= 2
    return v


def kernel(
    G, V, NS, EP, SEL, W,
    off_ref, sel_ref, series_hbm, out_ref,
    series_ref, load_sem, ep, inv, ep_far, inv_far, hot, part, slots, sums, sums_far,
    a_hi, a_lo, perm, send_far, send_near, send_emu, recv,
    gram, pair_in, pair_sum, pieces_in, last_in, summed, landed,
    slab_send, slab_recv, ep_send, ep_recv, sums_send, sums_recv,
    far_send, far_recv, last_send, last_recv, near_send, near_recv, emu_send, emu_recv,
    pair_send, pair_recv, rs_send, rs_recv, all_send, all_recv, fin_send, fin_recv,
):
    subj = lax.axis_index("subj")
    vox = lax.axis_index("vox")
    RUN = series_ref.shape[1]
    VL = series_ref.shape[2]
    ROWS = EP * TR
    SL = SEL // V
    NE = NS * EP
    chunks = VL // W
    R = pieces_of(G, V, NE)
    R2 = R // 2
    VR = V // R
    RP = G * NE // R
    PG = R // G
    HALF = G * NE // 2
    HG = G // 2
    HB = SEL // (2 * KB)
    KI = KB // HG
    T = HB * KI
    E1 = EP
    NR = NS * E1
    BR = recv.shape[2]
    starts = tuple(i * NR // 8 * 8 for i in range(KI))
    cuts = row_cuts(KI, NR, BR)
    groups = column_groups(chunks)
    shift = V // 2 + G // 2
    half = subj // HG
    core = lax.rem(subj, HG)
    far = [(1 - half) * HG + b for b in range(HG)]
    twin = (1 - half) * HG + core
    mates = [half * HG + lax.rem(core + d, HG) for d in range(1, HG)]

    barrier = pltpu.get_barrier_semaphore()
    for m in range(V - 1, 0, -1):
        pl.semaphore_signal(
            barrier, inc=1, device_id=(subj, flip(vox, m)), device_id_type=MESH,
        )
    for d in range(1, G):
        pl.semaphore_signal(
            barrier, inc=1, device_id=(lax.rem(subj + d, G), vox), device_id_type=MESH,
        )

    def load(s):
        return pltpu.make_async_copy(series_hbm.at[s], series_ref.at[s], load_sem.at[s])

    for s in range(NS):
        load(s).start()

    ids = jnp.zeros((SEL, 1), jnp.int32)
    which = iota((SEL, 1), 0)

    def chosen(kk, side):
        p = kk // HG * G + side * HG + kk % HG
        return sel_ref[(p + shift) % V * SL + p // V]

    for q in range(SEL):
        kk = q % (SEL // 2)
        swap = half == (0 if q < SEL // 2 else 1)
        ids = jnp.where(which == q, jnp.where(swap, chosen(kk, 1), chosen(kk, 0)), ids)
    picker = jnp.where(iota((SEL, VL), 1) + vox * VL == ids, 1.0, 0.0).astype(bf16)
    col = iota((TR, RUN), 1) - iota((TR, RUN), 0)
    pieces = []
    for s in range(NS):
        tiles = [
            jnp.where(col == off_ref[subj * NS + s, e], 1.0, 0.0) for e in range(EP)
        ]
        hot[s] = jnp.concatenate(tiles, axis=0).astype(bf16)
    for s in range(NS):
        load(s).wait()
        runs = lax.dot_general(
            picker, series_ref[s], (((1,), (1,)), ((), ())), preferred_element_type=f32
        )
        pieces.append(lax.dot_general(
            runs.astype(bf16), hot[s], (((1,), (1,)), ((), ())), preferred_element_type=f32
        ))
    joined = jnp.concatenate(pieces, axis=1)
    for h in range(2 * HB):
        part[h] = joined[h * KB:(h + 1) * KB].astype(bf16)

    def scale_of(x):
        x3 = x.reshape(EP, TR, W)
        total = jnp.sum(x3, axis=1)
        ssq = jnp.sum(x3 * x3, axis=1) - total * total * (1.0 / TR)
        return shrink_factor * lax.rsqrt(jnp.maximum(ssq, 0.0) + series_floor)

    def gather(c, carry):
        at = pl.ds(pl.multiple_of(c * W, W), W)
        for s in range(NS):
            x = jnp.dot(hot[s], series_ref[s, :, at], preferred_element_type=f32)
            ep[s, :, at] = x.astype(bf16)
            inv[s, :, at] = scale_of(x)
        return carry

    shared = pl.ds(0, W)
    gather(0, 0)
    after = max(chunks * C1 // 8, 1)
    pl.semaphore_wait(barrier, G + V - 2)

    def slab_copy(h, m):
        return pltpu.make_async_remote_copy(
            src_ref=part.at[h], dst_ref=slots.at[h, vox],
            send_sem=slab_send.at[h, m], recv_sem=slab_recv.at[h, m],
            device_id=(subj, flip(vox, m)), device_id_type=MESH,
        )

    def epoch_copy():
        return pltpu.make_async_remote_copy(
            src_ref=ep.at[:, :, shared], dst_ref=ep_far,
            send_sem=ep_send, recv_sem=ep_recv,
            device_id=(twin, vox), device_id_type=MESH,
        )

    def sums_copy(h):
        return pltpu.make_async_remote_copy(
            src_ref=sums.at[h], dst_ref=sums_far.at[h],
            send_sem=sums_send.at[h], recv_sem=sums_recv.at[h],
            device_id=(twin, vox), device_id_type=MESH,
        )

    for h in range(2 * HB):
        for m in range(V - 1, 0, -1):
            slab_copy(h, m).start()
        if h == 0:
            epoch_copy().start()

    out_row = iota((HG * BR, 1), 0)
    within = lax.rem(out_row, BR)
    item = lax.rem(within, NR)
    source = (item // E1 * EP + lax.rem(item, E1)) * KB + within // NR * HG + out_row // BR
    source = jnp.where(within < KI * NR, source, -1)
    perm[...] = jnp.where(source == iota((HG * BR, KB * NE), 1), 1.0, 0.0).astype(bf16)

    lax.fori_loop(1, after, gather, 0)

    same = iota((ROWS, ROWS), 0) // TR == iota((ROWS, ROWS), 1) // TR
    ones = jnp.where(same, 1.0, 0.0)
    pick_e = iota((EP, KB, ROWS), 2) // TR == iota((EP, KB, ROWS), 0)

    def standard_rows(h, slab):
        rows = jnp.concatenate(
            [slab[:, s * ROWS:(s + 1) * ROWS] for s in range(NS)], axis=0
        )
        mean = jnp.dot(
            rows.astype(bf16), ones.astype(bf16), preferred_element_type=f32
        ) * (1.0 / TR)
        centred = rows - mean
        ssq = jnp.dot(
            centred * centred, ones,
            precision=lax.Precision.HIGHEST, preferred_element_type=f32,
        )
        std = centred / jnp.sqrt(ssq + series_floor)
        hi = std.astype(bf16).astype(f32)
        lo = std - hi
        for s in range(NS):
            for value, where in ((hi, a_hi), (lo, a_lo)):
                block = value[s * KB:(s + 1) * KB]
                spread = jnp.where(pick_e, block[None], 0.0).reshape(EP * KB, ROWS)
                where[h, s] = spread.astype(bf16)

    def slab_sum(h):
        slab = part[h].astype(f32)
        for m in range(V - 1, 0, -1):
            slab_copy(h, m).wait_recv()
        for d in range(1, V):
            slab = slab + slots[h, lax.rem(vox + d, V)].astype(f32)
        return slab

    every = pl.ds(0, VL)

    def score(h, x_of, inv_of):
        parts = []
        for s in range(NS):
            x = x_of(s)
            corr = jnp.dot(a_hi[h, s], x, preferred_element_type=f32)
            corr = corr + jnp.dot(a_lo[h, s], x, preferred_element_type=f32)
            r = corr.reshape(EP, KB, W) * inv_of(s)[:, None, :]
            f = 0.5 * (jnp.log(1.0 + r) - jnp.log(1.0 - r))
            f = f - jnp.sum(f, axis=0, keepdims=True) * (1.0 / EP)
            var = jnp.sum(f * f, axis=0, keepdims=True) * (1.0 / EP)
            z = f * lax.rsqrt(var + spread_floor)
            parts.append(z.reshape(EP * KB, W).astype(bf16))
        z = jnp.concatenate(parts, axis=0)
        moved = jnp.dot(perm[...], z, preferred_element_type=f32)
        return moved.astype(bf16).reshape(HG, BR, W)

    def far_copy(h, b, sender, at):
        return pltpu.make_async_remote_copy(
            src_ref=send_far.at[h, b, :, at], dst_ref=recv.at[h, sender, :, at],
            send_sem=far_send.at[h, b], recv_sem=far_recv.at[h, lax.rem(sender, HG)],
            device_id=(far[b], vox), device_id_type=MESH,
        )

    P0 = len(groups) - 1

    def last_copy(n, b, sender, rows, at):
        rows = pl.ds(rows[0], rows[1] - rows[0])
        return pltpu.make_async_remote_copy(
            src_ref=send_far.at[HB - 1, b, rows, at],
            dst_ref=recv.at[HB - 1, sender, rows, at],
            send_sem=last_send.at[n, b], recv_sem=last_recv.at[n, lax.rem(sender, HG)],
            device_id=(far[b], vox), device_id_type=MESH,
        )

    def near_copy(h, d, sender, at):
        return pltpu.make_async_remote_copy(
            src_ref=send_near.at[h, lax.rem(mates[d - 1], HG), :, at],
            dst_ref=recv.at[h, sender, :, at],
            send_sem=near_send.at[h, d], recv_sem=near_recv.at[h, d],
            device_id=(mates[d - 1], vox), device_id_type=MESH,
        )

    def emu_copy(h, d, sender):
        return pltpu.make_async_remote_copy(
            src_ref=send_emu.at[h, lax.rem(mates[d - 1], HG)],
            dst_ref=recv.at[h, sender, :, shared],
            send_sem=emu_send.at[h, d], recv_sem=emu_recv.at[h, d],
            device_id=(mates[d - 1], vox), device_id_type=MESH,
        )

    beyond = pl.ds(W, VL - W)
    row_pieces = tuple(zip(cuts[:-1], cuts[1:]))
    last_plan = []
    for n, rows in enumerate(row_pieces):
        if rows[0] == rows[1]:
            continue
        if n < len(row_pieces) - 1:
            last_plan.append((n, rows, beyond))
        else:
            for g, (c0, c1) in enumerate(groups):
                last_plan.append((n + g, rows, pl.ds(c0 * W, (c1 - c0) * W)))

    for h in range(HB):
        slab = slab_sum(h)
        sums[h] = slab.astype(bf16)
        sums_copy(h).start()
        standard_rows(h, slab)

        def scores(c, carry, h=h):
            if h == 0 and after < chunks:
                @pl.when(c >= after)
                def _():
                    gather(c, 0)

            at = pl.ds(pl.multiple_of(c * W, W), W)
            send_far[h, :, :, at] = score(
                h, lambda s: ep[s, :, at], lambda s: inv[s, :, at]
            )
            for b in range(HG):
                if h < HB - 1:
                    far_copy(h, b, subj, at).start()
                elif cuts[1]:
                    last_copy(0, b, subj, row_pieces[0], at).start()
            return carry

        lax.fori_loop(1, chunks, scores, 0)
    for item_at in range(1, KI):
        closing = item_at == KI - 1
        for b in range(HG) if closing else range(HG - 1, -1, -1):
            for n, rows, at in last_plan:
                if rows == row_pieces[item_at]:
                    last_copy(n, b, subj, rows, at).start()

    for h in range(HB):
        standard_rows(HB + h, slab_sum(HB + h))

        def scores(c, carry, h=h):
            at = pl.ds(pl.multiple_of(c * W, W), W)
            send_near[h, :, :, at] = score(
                HB + h, lambda s: ep[s, :, at], lambda s: inv[s, :, at]
            )
            for d in range(1, HG):
                near_copy(h, d, subj, at).start()
            recv[h, subj, :, at] = send_near[h, core, :, at]
            return carry

        lax.fori_loop(0, chunks, scores, 0)

    epoch_copy().wait_recv()
    for s in range(NS):
        inv_far[s] = scale_of(ep_far[s].astype(f32))
    for h in range(HB):
        sums_copy(h).wait_recv()
        standard_rows(2 * HB + h, sums_far[h].astype(f32))
        send_emu[h] = score(2 * HB + h, lambda s: ep_far[s], lambda s: inv_far[s])
        for d in range(1, HG):
            emu_copy(h, d, twin).start()
        recv[h, twin, :, shared] = send_emu[h, core]

    def row_piece(r):
        return pl.ds(pl.multiple_of(r * RP, RP), RP)

    side, line = lax.rem(vox, 2), vox // 2
    pair = vox + 1 - 2 * side

    def pair_copy(t):
        rows = pl.ds(pl.multiple_of((1 - side) * HALF, HALF), HALF)
        return pltpu.make_async_remote_copy(
            src_ref=gram.at[t, rows], dst_ref=pair_in.at[t],
            send_sem=pair_send.at[t], recv_sem=pair_recv.at[t],
            device_id=(subj, pair), device_id_type=MESH,
        )

    def part_copy(t, m):
        to = flip(line, m)
        return pltpu.make_async_remote_copy(
            src_ref=pair_sum.at[t, row_piece(to // VR)], dst_ref=pieces_in.at[t, m - 1],
            send_sem=rs_send.at[t, m], recv_sem=rs_recv.at[t],
            device_id=(subj, to * 2 + side), device_id_type=MESH,
        )

    def all_parts(t):
        return pltpu.make_async_remote_copy(
            src_ref=pieces_in.at[t], dst_ref=pieces_in.at[t],
            send_sem=rs_send.at[t, 0], recv_sem=rs_recv.at[t],
            device_id=(subj, pair), device_id_type=MESH,
        )

    def piece_of(v):
        return lax.rem(v, 2) * R2 + v // 2 // VR

    def reduces(line):
        return lax.rem(line, VR) == 0

    TF = T - last_in.shape[0]

    def flat_copy(t, m):
        to = flip(vox, m)
        return pltpu.make_async_remote_copy(
            src_ref=gram.at[t, row_piece(piece_of(to))], dst_ref=last_in.at[t - TF, m - 1],
            send_sem=all_send.at[t - TF, m], recv_sem=all_recv.at[t - TF],
            device_id=(subj, to), device_id_type=MESH,
        )

    def flat_parts(t):
        return pltpu.make_async_remote_copy(
            src_ref=last_in.at[t - TF], dst_ref=last_in.at[t - TF],
            send_sem=all_send.at[t - TF, 0], recv_sem=all_recv.at[t - TF],
            device_id=(subj, pair), device_id_type=MESH,
        )

    piece = piece_of(vox)
    to_subj = piece // PG
    to_rows = lax.rem(piece, PG)

    def spot(t):
        p = t * G + subj
        return lax.rem(p + shift, V), p // V

    def final_copy(t):
        owner, local = spot(t)
        return pltpu.make_async_remote_copy(
            src_ref=summed.at[t], dst_ref=landed.at[local, to_rows],
            send_sem=fin_send.at[t], recv_sem=fin_recv.at[local, to_rows],
            device_id=(to_subj, owner), device_id_type=MESH,
        )

    def away(t):
        owner, local = spot(t)
        return jnp.logical_or(to_subj != subj, owner != vox)

    def middle(t):
        pair_copy(t).wait_recv()
        mine = pl.ds(pl.multiple_of(side * HALF, HALF), HALF)
        pair_sum[t] = gram[t, mine] + pair_in[t]
        for m in range(V // 2 - 1, 0, -1):
            @pl.when(reduces(flip(line, m)))
            def _():
                part_copy(t, m).start()

    def finish(t):
        @pl.when(reduces(line))
        def _():
            if t < TF:
                all_parts(t).wait_recv()
                total = pair_sum[t, row_piece(line // VR)]
                for d in range(V // 2 - 1):
                    total = total + pieces_in[t, d]
            else:
                flat_parts(t).wait_recv()
                total = gram[t, row_piece(piece)]
                for d in range(V - 1):
                    total = total + last_in[t - TF, d]
            total = total * (1.0 / (VL * V))
            summed[t] = total

            @pl.when(away(t))
            def _():
                final_copy(t).start()

            @pl.when(jnp.logical_not(away(t)))
            def _():
                landed[spot(t)[1], to_rows] = total

    def add_gram(t, c0, c1, fresh):
        h, i = t // KI, t % KI
        at = pl.ds(c0 * W, (c1 - c0) * W)
        rows = recv[h, :, starts[i]:starts[i] + NE, at].reshape(G * NE, -1)
        value = lax.dot_general(
            rows, rows, (((1,), (1,)), ((), ())), preferred_element_type=f32
        )
        gram[t] = value if fresh else gram[t] + value

    spans = tuple((c0 if g else 0, c1) for g, (c0, c1) in enumerate(groups))
    landed_rows = 0
    for t in range(T):
        h, i = t // KI, t % KI
        if i == 0:
            for d in range(1, HG):
                sender = half * HG + lax.rem(core - d + HG, HG)
                near_copy(h, d, sender, every).wait_recv()
                emu_copy(h, d, (1 - half) * HG + lax.rem(sender, HG)).wait_recv()
            landed_rows = 0
            if h < HB - 1:
                for b in range(HG):
                    far_copy(h, b, far[b], beyond).wait_recv()
                landed_rows = BR
        for g, (c0, c1) in enumerate(spans):
            for n, rows, at in last_plan:
                final = rows[1] == BR
                if final and (t < T - 1 or n != len(row_pieces) - 1 + g):
                    continue
                if h == HB - 1 and landed_rows < (i + 1) * NR and rows[0] == landed_rows:
                    for b in range(HG):
                        last_copy(n, b, far[b], rows, at).wait_recv()
                    if not final:
                        landed_rows = rows[1]
            add_gram(t, c0, c1, g == 0)
        if t < TF:
            pair_copy(t).start()
        else:
            for m in range(V - 1, 0, -1):
                @pl.when(reduces(flip(vox, m) // 2))
                def _():
                    flat_copy(t, m).start()
        if 0 < t <= TF:
            middle(t - 1)
        if 1 < t < T - 1:
            finish(t - 2)
    for t in range(max(T - 3, 0), T):
        finish(t)

    for local in range(SL):
        p = local * V + lax.rem(vox - shift + 2 * V, V)
        handler = lax.rem(p, G)
        for b in range(PG):
            owned = subj * PG + b
            source = lax.rem(owned, R2) * VR * 2 + owned // R2

            @pl.when(jnp.logical_or(handler != subj, source != vox))
            def _():
                pltpu.make_async_remote_copy(
                    src_ref=summed.at[0], dst_ref=landed.at[local, b],
                    send_sem=fin_send.at[0], recv_sem=fin_recv.at[local, b],
                    device_id=(subj, lax.rem(vox + 1, V)), device_id_type=MESH,
                ).wait_recv()
            out_ref[local, b * RP:(b + 1) * RP] = landed[local, b]

    for h in range(2 * HB):
        for m in range(1, V):
            slab_copy(h, m).wait_send()
    epoch_copy().wait_send()
    for h in range(HB):
        sums_copy(h).wait_send()
        for d in range(1, HG):
            near_copy(h, d, subj, every).wait_send()
            emu_copy(h, d, twin).wait_send()
        for b in range(HG):
            if h < HB - 1:
                far_copy(h, b, subj, beyond).wait_send()
            else:
                for n, rows, at in last_plan:
                    last_copy(n, b, subj, rows, at).wait_send()
    for t in range(T):
        if t >= TF:
            for m in range(1, V):
                @pl.when(reduces(flip(vox, m) // 2))
                def _():
                    flat_copy(t, m).wait_send()
        else:
            pair_copy(t).wait_send()
            for m in range(1, V // 2):
                @pl.when(reduces(flip(line, m)))
                def _():
                    part_copy(t, m).wait_send()

        @pl.when(jnp.logical_and(reduces(line), away(t)))
        def _():
            final_copy(t).wait_send()


def body(series, offsets, selected):
    G = lax.axis_size("subj")
    V = lax.axis_size("vox")
    NS, RUN, VL = series.shape
    EP = offsets.shape[1]
    SEL = selected.shape[0]
    W = 256
    NE = NS * EP
    ROWS = EP * TR
    HG = G // 2
    HB = SEL // (2 * KB)
    KI = KB // HG
    T = HB * KI
    NR = NS * EP
    BR = up8(KI * NR)
    SL = SEL // V
    R = pieces_of(G, V, NE)
    RP = G * NE // R
    chunks = VL // W
    plan = KI - 1 + len(column_groups(chunks))
    vm = pltpu.VMEM
    dma = pltpu.SemaphoreType.DMA
    return pl.pallas_call(
        functools.partial(kernel, G, V, NS, EP, SEL, W),
        out_shape=jax.ShapeDtypeStruct((SL, NE, G * NE), f32),
        in_specs=[
            pl.BlockSpec(memory_space=pltpu.SMEM),
            pl.BlockSpec(memory_space=pltpu.SMEM),
            pl.BlockSpec(memory_space=pl.ANY),
        ],
        out_specs=pl.BlockSpec(memory_space=pltpu.VMEM),
        scratch_shapes=[
            vm((NS, RUN, VL), bf16),
            dma((NS,)),
            vm((NS, ROWS, VL), bf16),
            vm((NS, EP, VL), f32),
            vm((NS, ROWS, W), bf16),
            vm((NS, EP, W), f32),
            vm((NS, ROWS, RUN), bf16),
            vm((2 * HB, KB, NS * ROWS), bf16),
            vm((2 * HB, V, KB, NS * ROWS), bf16),
            vm((HB, KB, NS * ROWS), bf16),
            vm((HB, KB, NS * ROWS), bf16),
            vm((3 * HB, NS, EP * KB, ROWS), bf16),
            vm((3 * HB, NS, EP * KB, ROWS), bf16),
            vm((HG * BR, KB * NE), bf16),
            vm((HB, HG, BR, VL), bf16),
            vm((HB, HG, BR, VL), bf16),
            vm((HB, HG, BR, W), bf16),
            vm((HB, G, BR, VL), bf16),
            vm((T, G * NE, G * NE), f32),
            vm((T, G * NE // 2, G * NE), f32),
            vm((T, G * NE // 2, G * NE), f32),
            vm((T, V // 2 - 1, RP, G * NE), f32),
            vm((min(3, T), V - 1, RP, G * NE), f32),
            vm((T, RP, G * NE), f32),
            vm((SL, R // G, RP, G * NE), f32),
            dma((2 * HB, V)),
            dma((2 * HB, V)),
            dma,
            dma,
            dma((HB,)),
            dma((HB,)),
            dma((HB, HG)),
            dma((HB, HG)),
            dma((plan, HG)),
            dma((plan, HG)),
            dma((HB, HG)),
            dma((HB, HG)),
            dma((HB, HG)),
            dma((HB, HG)),
            dma((T,)),
            dma((T,)),
            dma((T, V // 2)),
            dma((T,)),
            dma((min(3, T), V)),
            dma((min(3, T),)),
            dma((T,)),
            dma((SL, R // G)),
        ],
        compiler_params=pltpu.CompilerParams(
            collective_id=0, has_side_effects=True, vmem_limit_bytes=56 * 1024 * 1024
        ),
    )(offsets, selected, series)


def solution(mesh):
    placed = (P("subj", None, "vox"), P(), P())
    return jax.shard_map(
        body, mesh=mesh, in_specs=placed, out_specs=P("vox", "subj", None), check_vma=False
    )
```

profile of v0, /device:TPU:15, one launch (start us, length us, event | category | flops | bytes accessed | tf_op | source)
XLA Modules:
  0.0 57.4 jit_solution(9676896296809512607)
XLA Ops:
  0.0 55.8 %shard_map.37 = f32[2,48,192]{2,1,0:T(8,128)} custom-call(s32[16,12]{1,0:T(8,128)} %off_ref.1, s32[16]{0:T(128)} %sel_ref.1, bf16[4,256,2048]{2,1,0:T(8,128)(2,1)} %series_hbm.1), custom_call_target="tpu_custom_call" | custom-call | tf_op jit(solution)/shard_map/pallas_call | solution.py:575
  55.8 1.5 %copy.5 = f32[2,48,192]{2,1,0:T(8,128)} copy(f32[2,48,192]{2,1,0:T(8,128)} %shard_map.37) | data formatting | bytes 147456
where the time goes:
time: 58.3 us; the launch traced here: 57.4 us
  Pallas kernels  55.8 us (96%)
  local copies, waits for them, and re-layouts  1.54 us (3%)
    pallas_call x1, Pallas kernels, body(): pl.pallas_call(functools.partial(kernel, G, V, NS, EP, SEL, W), out_shape...  55.8 us
    unnamed x1, local copies, waits for them, and re-layouts  1.54 us

commit v1 on v0

--- a/solution.py
+++ b/solution.py
@@ -56,7 +56,7 @@
     off_ref, sel_ref, series_hbm, out_ref,
     series_ref, load_sem, ep, inv, ep_far, inv_far, hot, part, slots, sums, sums_far,
     a_hi, a_lo, perm, send_far, send_near, send_emu, recv,
-    gram, pair_in, pair_sum, pieces_in, last_in, summed, landed,
+    gram, packed, pair_in, pair_sum, pieces_in, last_in, summed, landed,
     slab_send, slab_recv, ep_send, ep_recv, sums_send, sums_recv,
     far_send, far_recv, last_send, last_recv, near_send, near_recv, emu_send, emu_recv,
     pair_send, pair_recv, rs_send, rs_recv, all_send, all_recv, fin_send, fin_recv,
@@ -388,10 +388,21 @@
     def flat_copy(t, m):
         to = flip(vox, m)
         return pltpu.make_async_remote_copy(
-            src_ref=gram.at[t, row_piece(piece_of(to))], dst_ref=last_in.at[t - TF, m - 1],
+            src_ref=packed.at[t - TF, piece_of(to)], dst_ref=last_in.at[t - TF, m - 1],
             send_sem=all_send.at[t - TF, m], recv_sem=all_recv.at[t - TF],
             device_id=(subj, to), device_id_type=MESH,
         )
+
+    LEFT = G * NE // 128 * 128
+    REST = G * NE - LEFT
+    TALL = packed.shape[2] - RP
+
+    def pack(t):
+        for p in range(R):
+            rows = gram[t, p * RP:(p + 1) * RP]
+            packed[t - TF, p, :RP] = rows[:, :LEFT]
+            packed[t - TF, p, RP:, :REST] = rows[:TALL, LEFT:]
+            packed[t - TF, p, RP:2 * RP - TALL, REST:2 * REST] = rows[TALL:, LEFT:]
 
     def flat_parts(t):
         return pltpu.make_async_remote_copy(
@@ -439,10 +450,15 @@
                     total = total + pieces_in[t, d]
             else:
                 flat_parts(t).wait_recv()
-                total = gram[t, row_piece(piece)]
+                total = packed[t - TF, piece]
                 for d in range(V - 1):
                     total = total + last_in[t - TF, d]
             total = total * (1.0 / (VL * V))
+            if t >= TF:
+                rest = jnp.concatenate(
+                    [total[RP:, :REST], total[RP:2 * RP - TALL, REST:2 * REST]], axis=0
+                )
+                total = jnp.concatenate([total[:RP], rest], axis=1)
             summed[t] = total
 
             @pl.when(away(t))
@@ -490,6 +506,7 @@
         if t < TF:
             pair_copy(t).start()
         else:
+            pack(t)
             for m in range(V - 1, 0, -1):
                 @pl.when(reduces(flip(vox, m) // 2))
                 def _():
@@ -601,10 +618,11 @@
             vm((HB, HG, BR, W), bf16),
             vm((HB, G, BR, VL), bf16),
             vm((T, G * NE, G * NE), f32),
+            vm((min(2, T), R, RP + up8(-(-RP // 2)), G * NE // 128 * 128), f32),
             vm((T, G * NE // 2, G * NE), f32),
             vm((T, G * NE // 2, G * NE), f32),
             vm((T, V // 2 - 1, RP, G * NE), f32),
-            vm((min(3, T), V - 1, RP, G * NE), f32),
+            vm((min(2, T), V - 1, RP + up8(-(-RP // 2)), G * NE // 128 * 128), f32),
             vm((T, RP, G * NE), f32),
             vm((SL, R // G, RP, G * NE), f32),
             dma((2 * HB, V)),
@@ -625,8 +643,8 @@
             dma((T,)),
             dma((T, V // 2)),
             dma((T,)),
-            dma((min(3, T), V)),
-            dma((min(3, T),)),
+            dma((min(2, T), V)),
+            dma((min(2, T),)),
             dma((T,)),
             dma((SL, R // G)),
         ],

time: 58.3 us -> 58.1 us (level)
  no operation moved by 1% of the time
where the time goes in v1:
time: 58.1 us; the launch traced here: 57 us
  Pallas kernels  55.4 us (95%)
  local copies, waits for them, and re-layouts  1.54 us (3%)
    pallas_call x1, Pallas kernels, body(): pl.pallas_call(functools.partial(kernel, G, V, NS, EP, SEL, W), out_shape...  55.4 us
    unnamed x1, local copies, waits for them, and re-layouts  1.54 us

profile of v1, /device:TPU:15, one launch (start us, length us, event | category | flops | bytes accessed | tf_op | source)
XLA Modules:
  0.0 57.0 jit_solution(2667165475719869452)
XLA Ops:
  0.0 55.4 %shard_map.37 = f32[2,48,192]{2,1,0:T(8,128)} custom-call(s32[16,12]{1,0:T(8,128)} %off_ref.1, s32[16]{0:T(128)} %sel_ref.1, bf16[4,256,2048]{2,1,0:T(8,128)(2,1)} %series_hbm.1), custom_call_target="tpu_custom_call" | custom-call | tf_op jit(solution)/shard_map/pallas_call | solution.py:592
  55.4 1.5 %copy.5 = f32[2,48,192]{2,1,0:T(8,128)} copy(f32[2,48,192]{2,1,0:T(8,128)} %shard_map.37) | data formatting | bytes 147456
